TPU v7x, 128 devices: a whole 4x4x4 slice. The times are simulated.
128 devices in a mesh: grp: 4 (over y_hi, core), row: 32 (over y_lo, z, x).
Axes of the slice: x: 4, y: 4 (y_hi: 2, y_lo: 2; y = y_hi * 2 + y_lo), z: 4, core: 2. Of those that a mesh axis runs over, the one named last changes fastest.
Arguments:
- landmarks: bfloat16 [4096, 1024], P(('grp', 'row')), may hold values from -6.5 to 6.5
- initial_basis: bfloat16 [4096, 256], P(('grp', 'row')), may hold values from -0.09375 to 0.09375
- points: bfloat16 [131072, 1024], P(('grp', 'row')), may hold values from -6.5 to 6.5
Outputs:
- basis: float32 [4096, 256], P(('grp', 'row'))
- coords: float32 [131072, 256], P(('grp', 'row'))
All inputs are finite; a program needn't handle non-finite values.
Results may differ from a plain program's by a relative error of at most 0.0057.
Values may be sent and summed in bfloat16 or wider, within the bound.
A program may use at most 128 MiB of HBM per device.

v0:
```python
import math
import jax
import jax.numpy as jnp
from jax import lax
from jax.sharding import PartitionSpec as P

ITERS = 2
spread = 0.25


def laid_out(blocks, dim):
    blocks = jnp.moveaxis(blocks, 0, dim)
    shape = blocks.shape
    return blocks.reshape(*shape[:dim], shape[dim] * shape[dim + 1], *shape[dim + 2 :])


def copy_for_each(x, axis):
    devices = lax.axis_size(axis)
    return lax.all_to_all(jnp.broadcast_to(x[None], (devices, *x.shape)), axis, 0, 0, tiled=True)


def collect(x, axis, dim):
    return laid_out(copy_for_each(x, axis), dim)


def of_everyone(x, axis):
    return copy_for_each(x, axis).sum(axis=0)


def in_blocks(x, dim, devices):
    shape = x.shape
    blocks = x.reshape(*shape[:dim], devices, shape[dim] // devices, *shape[dim + 1 :])
    return jnp.moveaxis(blocks, dim, 0)


def sum_at_owner(x, axis, dim):
    devices = lax.axis_size(axis)
    blocks = lax.all_to_all(in_blocks(x, dim, devices), axis, 0, 0, tiled=True)
    return jnp.sum(blocks, axis=0)


def side_by_side(arrays, axis, dim, along):
    columns = [a.reshape(*a.shape[:along], -1) for a in arrays]
    both = jnp.concatenate(columns, axis=along)
    out, at, gathered = (lax.psum_scatter(both, axis, scatter_dimension=dim, tiled=True), 0, [])
    for a, column in zip(arrays, columns):
        share = out[..., at : at + column.shape[along]]
        gathered.append(share.reshape(*share.shape[:along], *a.shape[along:]))
        at += column.shape[along]
    return tuple(gathered)


def squared_rows(rows):
    return jnp.sum(jnp.square(rows.astype(jnp.float32)), axis=1)


def pair_kernel(left, right):
    inner = lax.dot_general(
        left, right, (((1,), (1,)), ((), ())), preferred_element_type=jnp.float32
    )
    dist = squared_rows(left)[:, None] + squared_rows(right)[None, :] - 2.0 * inner
    return jnp.exp(-dist / (spread * left.shape[1]))


def point_terms(anchors, spectral_rows, members, member_sq):
    inner = lax.dot_general(
        anchors, members, (((1,), (1,)), ((), ())), preferred_element_type=jnp.float32
    )
    dist = squared_rows(anchors)[:, None] + member_sq[None, :] - 2.0 * inner
    kernel_part = jnp.exp(-dist / (spread * anchors.shape[1]))
    degree_part = jnp.sum(kernel_part, axis=0)
    numer_part = lax.dot_general(
        kernel_part.astype(jnp.bfloat16),
        spectral_rows,
        (((0,), (0,)), ((), ())),
        preferred_element_type=jnp.float32,
    )
    return (numer_part, degree_part)


def body(landmarks, initial_basis, points):
    local_rows = landmarks.shape[0]
    total = local_rows * lax.axis_size("grp") * lax.axis_size("row")
    row_index = lax.axis_index("row")
    group_rows = lax.all_gather(landmarks, "row", axis=0, tiled=True)
    cross_rows = collect(landmarks, "grp", 0)
    land_kernel = pair_kernel(group_rows, cross_rows)
    group_degree = of_everyone(jnp.sum(land_kernel, axis=1), "row")
    own_degree = lax.dynamic_slice_in_dim(group_degree, row_index * local_rows, local_rows, 0)
    cross_degree = collect(own_degree, "grp", 0)
    row_scale = 1.0 / jnp.sqrt(group_degree)
    column_scale = 1.0 / jnp.sqrt(cross_degree)
    affinity = (land_kernel * row_scale[:, None] * column_scale[None, :]).astype(jnp.bfloat16)
    current = initial_basis
    for step in range(ITERS):
        cross_basis = collect(current, "grp", 0)
        image = sum_at_owner(
            jnp.dot(affinity, cross_basis, preferred_element_type=jnp.float32), "row", 0
        )
        gram = lax.psum(jnp.dot(image.T, image, precision=lax.Precision.HIGHEST), ("grp", "row"))
        lower = jnp.linalg.cholesky(gram)
        ortho = jax.scipy.linalg.solve_triangular(lower, image.T, lower=True).T
        current = ortho.astype(jnp.bfloat16)
    lam = jnp.diagonal(lower)
    own_scale = 1.0 / jnp.sqrt(own_degree)
    spectral = (ortho * own_scale[:, None] / lam[None, :]).astype(jnp.bfloat16)
    group_spectral = collect(spectral, "row", 0)
    cross_points = lax.all_gather(points, "grp", axis=0, tiled=True)
    numer_part, degree_part = point_terms(
        group_rows, group_spectral, cross_points, squared_rows(cross_points)
    )
    numer, degree = side_by_side((numer_part, degree_part), "grp", 0, 1)
    coords = numer / jnp.sqrt(degree)[:, None] * math.sqrt(total)
    return (ortho, coords)


def solution(mesh):
    in_specs = (P(("grp", "row"), None), P(("grp", "row"), None), P(("grp", "row"), None))
    out_specs = (P(("grp", "row"), None), P(("grp", "row"), None))
    return jax.shard_map(body, mesh=mesh, in_specs=in_specs, out_specs=out_specs, check_vma=False)
```

profile of v0, /device:TPU:1, one launch (start us, length us, event | category | flops | bytes accessed | tf_op | source)
XLA Modules:
  0.0 810.1 jit_solution(4297087186044760652)
XLA Ops:
  9.6 12.2 %all_to_all.42 = bf16[4,32,1024]{2,1,0:T(8,128)(2,1)S(1)} all-to-all(bf16[4,32,1024]{2,1,0:T(8,128)(2,1)S(1)} %broadcast_in_dim.14), channel_id=1, replica_groups=mesh['grp'=4,'row'=32] {'grp'}, dimensions={0} | all-to-all | bytes 524288 | tf_op jit(solution)/shard_map/all_to_all | solution.py:19
  22.0 122.9 %all-gather.3.cloned.1.call-done = bf16[1024,1024]{1,0:T(8,128)(2,1)} async-done(((bf16[32,1024]{1,0:T(8,128)(2,1)}), bf16[1024,1024]{1,0:T(8,128)(2,1)}) %all-gather.3.cloned.1.call-update) | async-done | bytes 2097168 | tf_op jit(solution)/shard_map/all_gather | solution.py:85
  150.1 6.2 all-to-all-start.1
  156.4 7.3 all-to-all-done.1
  164.4 28.1 %all-to-all-start.2 = ((f32[4,1,32]{2,1,0:T(1,128)}), f32[4,1,32]{2,1,0:T(1,128)S(1)}, u32[]{:S(2)}, u32[]{:S(2)}) async-start(f32[4,1,32]{2,1,0:T(1,128)} %broadcast_in_dim.16), calls=%async_computation.2 | async-start | bytes 4096 | tf_op jit(solution)/shard_map/all_to_all | solution.py:19
  192.6 4.5 all-to-all-done.2
  207.4 19.0 %all_to_all.44 = f32[32,32,256]{2,1,0:T(8,128)S(1)} all-to-all(f32[32,32,256]{2,1,0:T(8,128)S(1)} %fusion.39), channel_id=1, replica_groups=mesh['grp'=4,'row'=32] {'row'}, dimensions={0} | all-to-all | bytes 2097152 | tf_op jit(solution)/shard_map/all_to_all | solution.py:38
  228.2 140.3 %all-reduce.4.cloned.1.call-done = f32[256,256]{0,1:T(8,128)} async-done(((f32[256,256]{0,1:T(8,128)}), f32[256,256]{0,1:T(8,128)}) %all-reduce.4.cloned.1.call-update) | async-done | bytes 262160 | tf_op jit(solution)/shard_map/psum | solution.py:100
  370.6 11.7 %cholesky.130 = f32[128,128]{1,0:T(8,128)S(1)} custom-call(f32[128,128]{1,0:T(8,128)S(1)} %cholesky.194), custom_call_target="Cholesky" | custom-call | tf_op jit(solution)/shard_map/jit(cholesky)/cholesky | solution.py:101
  382.4 9.8 %custom-call.15 = f32[1,128,128]{1,2,0:T(8,128)S(1)} custom-call(f32[1,128,128]{2,1,0:T(8,128)S(1)} %get-tuple-element.63), custom_call_target="InvertDiagBlocksLowerTriangular" | custom-call | tf_op jit(solution)/shard_map/jit(cholesky)/cholesky | solution.py:101
  392.7 11.7 %cholesky.147 = f32[128,128]{1,0:T(8,128)S(1)} custom-call(f32[128,128]{1,0:T(8,128)S(1)} %convolution_subtract_fusion.1), custom_call_target="Cholesky" | custom-call | tf_op jit(solution)/shard_map/jit(cholesky)/cholesky | solution.py:101
  410.8 19.7 %custom-call.16 = f32[2,128,128]{1,2,0:T(8,128)S(1)} custom-call(f32[2,128,128]{2,1,0:T(8,128)S(1)} %get-tuple-element.18), custom_call_target="InvertDiagBlocksLowerTriangular" | custom-call | tf_op jit(solution)/shard_map/jit(_solve_triangular)/triangular_solve | solution.py:102
  431.1 8.7 %all_to_all.43 = bf16[4,32,256]{2,1,0:T(8,128)(2,1)S(1)} all-to-all(bf16[4,32,256]{2,1,0:T(8,128)(2,1)S(1)} %broadcast_in_dim.18), channel_id=1, replica_groups=mesh['grp'=4,'row'=32] {'grp'}, dimensions={0} | all-to-all | bytes 131072 | tf_op jit(solution)/shard_map/all_to_all | solution.py:19
  440.1 19.6 %all_to_all.45 = f32[32,32,256]{2,1,0:T(8,128)S(1)} all-to-all(f32[32,32,256]{2,1,0:T(8,128)S(1)} %fusion.41), channel_id=1, replica_groups=mesh['grp'=4,'row'=32] {'row'}, dimensions={0} | all-to-all | bytes 2097152 | tf_op jit(solution)/shard_map/all_to_all | solution.py:38
  461.5 183.1 %all-reduce.6.cloned.1.call-done = f32[256,256]{0,1:T(8,128)} async-done(((f32[256,256]{0,1:T(8,128)}), f32[256,256]{0,1:T(8,128)}) %all-reduce.6.cloned.1.call-update) | async-done | bytes 262160 | tf_op jit(solution)/shard_map/psum | solution.py:100
  646.6 11.7 %cholesky.164 = f32[128,128]{1,0:T(8,128)S(1)} custom-call(f32[128,128]{1,0:T(8,128)S(1)} %cholesky.197), custom_call_target="Cholesky" | custom-call | tf_op jit(solution)/shard_map/jit(cholesky)/cholesky | solution.py:101
  658.4 9.8 %custom-call.17 = f32[1,128,128]{1,2,0:T(8,128)S(1)} custom-call(f32[1,128,128]{2,1,0:T(8,128)S(1)} %get-tuple-element.59), custom_call_target="InvertDiagBlocksLowerTriangular" | custom-call | tf_op jit(solution)/shard_map/jit(cholesky)/cholesky | solution.py:101
  668.7 11.7 %cholesky.181 = f32[128,128]{1,0:T(8,128)S(1)} custom-call(f32[128,128]{1,0:T(8,128)S(1)} %convolution_subtract_fusion), custom_call_target="Cholesky" | custom-call | tf_op jit(solution)/shard_map/jit(cholesky)/cholesky | solution.py:101
  687.3 19.7 %custom-call.18 = f32[2,128,128]{1,2,0:T(8,128)S(1)} custom-call(f32[2,128,128]{2,1,0:T(8,128)S(1)} %get-tuple-element.19), custom_call_target="InvertDiagBlocksLowerTriangular" | custom-call | tf_op jit(solution)/shard_map/jit(_solve_triangular)/triangular_solve | solution.py:102
  711.4 5.0 all-to-all-start.7
  716.5 5.2 multiply_reduce_fusion
  722.2 13.9 %fusion = (f32[4096]{0:T(1024)S(1)}, f32[1024,4096]{1,0:T(8,128)}) fusion(f32[4096]{0:T(1024)S(1)} %multiply_reduce_fusion, f32[1024]{0:T(1024)S(1)} %multiply_reduce_fusion.1, bf16[1024,1024]{1,0:T(8,128)(2,1)S(1)} %copy-done.1, bf16[4096,1024]{1,0:T(8,128)(2,1)S(1)} %copy-done), kind=kOutput, calls=%fused_computation.7 | convolution fusion | flops 8615096320 | bytes 27299840 | tf_op jit(solution)/shard_map/dot_general | solution.py:66
  736.1 8.2 %fusion.2 = f32[4096,256]{0,1:T(8,128)S(1)} fusion(bf16[1024,256]{1,0:T(8,128)(2,1)S(1)} %bitcast.102, f32[1024,4096]{1,0:T(8,128)} %get-tuple-element.71, f32[4096]{0:T(1024)S(1)} %multiply_reduce_fusion, f32[1024]{0:T(1024)S(1)} %multiply_reduce_fusion.1), kind=kOutput, calls=%fused_computation.9 | convolution fusion | flops 2172649472 | bytes 21516288 | tf_op jit(solution)/shard_map/dot_general | solution.py:72
  746.6 52.7 %reduce-scatter.2.cloned.1.call-done = f32[1024,257]{0,1:T(8,128)} async-done(((f32[4096,257]{0,1:T(8,128)}), f32[1024,257]{0,1:T(8,128)}) %reduce-scatter.2.cloned.1.call-update) | async-done | bytes 1052688 | tf_op jit(solution)/shard_map/reduce_scatter | solution.py:45
  (93 shorter events, 56.9 us)
Async XLA Ops:
  8.0 137.0 %all-gather.3.cloned.1.call-start = ((), (), s32[]{:S(2)}) async-start(), calls=%async_computation.9 | async-start | bytes 2162688 | tf_op jit(solution)/shard_map/all_gather | solution.py:85
  150.1 13.5 %all-to-all-start.1 = ((f32[32,1,1024]{2,1,0:T(1,128)}), f32[32,1,1024]{2,1,0:T(1,128)S(1)}, u32[]{:S(2)}, u32[]{:S(2)}) async-start(f32[32,1,1024]{2,1,0:T(1,128)} %broadcast_in_dim.15), calls=%async_computation.1 | async-start | bytes 262144 | tf_op jit(solution)/shard_map/all_to_all | solution.py:19
  164.4 32.6 %all-to-all-start.2 = ((f32[4,1,32]{2,1,0:T(1,128)}), f32[4,1,32]{2,1,0:T(1,128)S(1)}, u32[]{:S(2)}, u32[]{:S(2)}) async-start(f32[4,1,32]{2,1,0:T(1,128)} %broadcast_in_dim.16), calls=%async_computation.2 | async-start | bytes 4096 | tf_op jit(solution)/shard_map/all_to_all | solution.py:19
  198.4 8.7 %all-to-all-start.3 = ((bf16[4,32,256]{2,1,0:T(8,128)(2,1)}), bf16[4,32,256]{2,1,0:T(8,128)(2,1)S(1)}, u32[]{:S(2)}, u32[]{:S(2)}) async-start(bf16[4,32,256]{2,1,0:T(8,128)(2,1)} %broadcast_in_dim.17), calls=%async_computation.3 | async-start | bytes 131072 | tf_op jit(solution)/shard_map/all_to_all | solution.py:19
  202.4 166.1 %all-reduce.4.cloned.1.call-start = ((), (), s32[]{:S(2)}) async-start(), calls=%async_computation.10 | async-start | bytes 524288 | tf_op jit(solution)/shard_map/psum | solution.py:100
  227.7 416.9 %all-reduce.6.cloned.1.call-start = ((), (), s32[]{:S(2)}) async-start(), calls=%async_computation.11 | async-start | bytes 524288 | tf_op jit(solution)/shard_map/psum | solution.py:100
  460.9 255.6 %all-gather.5.cloned.1.call-start = ((), (), s32[]{:S(2)}) async-start(), calls=%async_computation.12 | async-start | bytes 10485760 | tf_op jit(solution)/shard_map/all_gather | solution.py:108
  461.5 260.3 %copy-start.1 = (bf16[1024,1024]{1,0:T(8,128)(2,1)S(1)}, bf16[1024,1024]{1,0:T(8,128)(2,1)}, u32[]{:S(2)}) copy-start(bf16[1024,1024]{1,0:T(8,128)(2,1)} %all-gather.3.cloned.1.call-done) | copy-start | bytes 6291460
  711.4 24.7 %all-to-all-start.7 = ((bf16[32,32,256]{2,1,0:T(8,128)(2,1)}), bf16[32,32,256]{2,1,0:T(8,128)(2,1)S(1)}, u32[]{:S(2)}, u32[]{:S(2)}) async-start(bf16[32,32,256]{2,1,0:T(8,128)(2,1)} %broadcast_in_dim.19), calls=%async_computation.7 | async-start | bytes 1048576 | tf_op jit(solution)/shard_map/all_to_all | solution.py:19
  716.4 83.0 %reduce-scatter.2.cloned.1.call-start = ((), (), s32[]{:S(2)}) async-start(), calls=%async_computation.13 | async-start | bytes 5406720 | tf_op jit(solution)/shard_map/reduce_scatter | solution.py:45
  716.5 5.8 copy-start
Sparse Core Ops, SparseCore 0:
  10.4 134.4 all-gather.2
  227.8 140.6 all-reduce.3
  461.0 183.4 all-reduce.5
Sparse Core Ops, SparseCore 1:
  463.0 60.4 all-gather.4
  746.7 52.6 reduce-scatter.1
where the time goes:
time: 814 us; the launch traced here: 810 us
  waiting for transfers between devices  517 us (64%)
  other arithmetic  122 us (15%)
  blocking collectives  59.6 us (7%)
  starting transfers between devices  43.9 us (5%)
  matrix products  29.3 us (4%)
  local copies, waits for them, and re-layouts  19.8 us (2%)
  between operations  18.4 us (2%)
    psum x2, waiting for transfers between devices, body(): lax.psum(jnp.dot(image.T, image, precision=lax.Precision.HIGHEST), ('grp'...  323 us
    all_gather x1, waiting for transfers between devices, body(): group_rows = lax.all_gather(landmarks, 'row', axis=0, tiled=True)  123 us
    another operation x13, other arithmetic, body(): lower = jnp.linalg.cholesky(gram)  68.6 us
    reduce_scatter x1, waiting for transfers between devices, side_by_side(): lax.psum_scatter(both, axis, scatter_dimension=dim, tiled=True)  52.7 us
    all_to_all x4, starting transfers between devices, copy_for_each(): lax.all_to_all(jnp.broadcast_to(x[None], (devices, *x.shape)), axis, 0, 0...  43.2 us
    another operation x5, other arithmetic, body(): ortho = jax.scipy.linalg.solve_triangular(lower, image.T, lower=True).T  39.4 us
    all_to_all x2, blocking collectives, sum_at_owner(): blocks = lax.all_to_all(in_blocks(x, dim, devices), axis, 0, 0, tiled=True)  38.6 us
    all_to_all x2, blocking collectives, copy_for_each(): lax.all_to_all(jnp.broadcast_to(x[None], (devices, *x.shape)), axis, 0, 0...  20.9 us
  transfers between devices with their start and end apart: 9, of which 7 were waited for; matrix products, arithmetic and copies ran while one was open for 11% of the time, Pallas kernels for 0%

commit v1 on v0

--- a/solution.py
+++ b/solution.py
@@ -6,6 +6,12 @@
 
 ITERS = 2
 spread = 0.25
+
+
+def summed_here(block, mesh_axis):
+    shards = lax.all_gather(block, mesh_axis, axis=0, tiled=False)
+    total = shards.sum(axis=0)
+    return total
 
 
 def laid_out(blocks, dim):
@@ -97,7 +103,7 @@
         image = sum_at_owner(
             jnp.dot(affinity, cross_basis, preferred_element_type=jnp.float32), "row", 0
         )
-        gram = lax.psum(jnp.dot(image.T, image, precision=lax.Precision.HIGHEST), ("grp", "row"))
+        gram = summed_here(jnp.dot(image.T, image, precision=lax.Precision.HIGHEST), ("grp", "row"))
         lower = jnp.linalg.cholesky(gram)
         ortho = jax.scipy.linalg.solve_triangular(lower, image.T, lower=True).T
         current = ortho.astype(jnp.bfloat16)

time: 814 us -> 1200 us (1.47)
  waiting for transfers between devices: 517 us -> 869 us
  other arithmetic: 122 us -> 156 us
    all_gather x0 -> x2, waiting for transfers between devices: none -> 675 us  [summed_here(): shards = lax.all_gather(block, mesh_axis, axis=0, tiled=False)]
    psum x2 -> x0, waiting for transfers between devices: 323 us -> none  [body(): lax.psum(jnp.dot(image.T, image, precision=lax.Precision.HIGHEST), ('grp'...]
    reduce_sum x0 -> x2, other arithmetic: none -> 24.3 us  [summed_here(): total = shards.sum(axis=0)]
  transfers between devices with their start and end apart: 9 -> 9, of which waited for: 7 -> 7; matrix products, arithmetic and copies ran while one was open for 11% -> 9% of each run, Pallas kernels for 0% -> 0%
where the time goes in v1:
time: 1200 us
  waiting for transfers between devices  869 us (72%)
  other arithmetic  156 us (13%)
  blocking collectives  62.1 us (5%)
  starting transfers between devices  46.2 us (4%)
  matrix products  31 us (3%)
  local copies, waits for them, and re-layouts  17.5 us (1%)
  between operations  17 us (1%)
    all_gather x2, waiting for transfers between devices, summed_here(): shards = lax.all_gather(block, mesh_axis, axis=0, tiled=False)  675 us
    all_gather x1, waiting for transfers between devices, body(): group_rows = lax.all_gather(landmarks, 'row', axis=0, tiled=True)  123 us
    another operation x13, other arithmetic, body(): lower = jnp.linalg.cholesky(gram)  68.6 us
    reduce_scatter x1, waiting for transfers between devices, side_by_side(): lax.psum_scatter(both, axis, scatter_dimension=dim, tiled=True)  53.3 us
    another operation x5, other arithmetic, body(): ortho = jax.scipy.linalg.solve_triangular(lower, image.T, lower=True).T  50.8 us
    all_to_all x4, starting transfers between devices, copy_for_each(): lax.all_to_all(jnp.broadcast_to(x[None], (devices, *x.shape)), axis, 0, 0...  45.7 us
    all_to_all x2, blocking collectives, sum_at_owner(): blocks = lax.all_to_all(in_blocks(x, dim, devices), axis, 0, 0, tiled=True)  41.4 us
    reduce_sum x2, other arithmetic, summed_here(): total = shards.sum(axis=0)  24.3 us
  transfers between devices with their start and end apart: 9, of which 7 were waited for; matrix products, arithmetic and copies ran while one was open for 9% of the time, Pallas kernels for 0%

profile of v1, /device:TPU:1, one launch (start us, length us, event | category | flops | bytes accessed | tf_op | source)
XLA Modules:
  0.0 1198.7 jit_solution(1376467979749651863)
XLA Ops:
  8.8 12.2 %all_to_all.42 = bf16[4,32,1024]{2,1,0:T(8,128)(2,1)S(1)} all-to-all(bf16[4,32,1024]{2,1,0:T(8,128)(2,1)S(1)} %broadcast_in_dim.14), channel_id=1, replica_groups=mesh['grp'=4,'row'=32] {'grp'}, dimensions={0} | all-to-all | bytes 524288 | tf_op jit(solution)/shard_map/all_to_all | solution.py:25
  21.2 122.9 %all-gather.7.cloned.1.call-done = bf16[1024,1024]{1,0:T(8,128)(2,1)} async-done(((bf16[32,1024]{1,0:T(8,128)(2,1)}), bf16[1024,1024]{1,0:T(8,128)(2,1)}) %all-gather.7.cloned.1.call-update) | async-done | bytes 2097168 | tf_op jit(solution)/shard_map/all_gather | solution.py:91
  149.3 6.2 all-to-all-start.1
  155.6 7.3 all-to-all-done.1
  163.6 28.1 %all-to-all-start.2 = ((f32[4,1,32]{2,1,0:T(1,128)}), f32[4,1,32]{2,1,0:T(1,128)S(1)}, u32[]{:S(2)}, u32[]{:S(2)}) async-start(f32[4,1,32]{2,1,0:T(1,128)} %broadcast_in_dim.16), calls=%async_computation.2 | async-start | bytes 4096 | tf_op jit(solution)/shard_map/all_to_all | solution.py:25
  206.6 19.0 %all_to_all.44 = f32[32,32,256]{2,1,0:T(8,128)S(1)} all-to-all(f32[32,32,256]{2,1,0:T(8,128)S(1)} %fusion.39), channel_id=1, replica_groups=mesh['grp'=4,'row'=32] {'row'}, dimensions={0} | all-to-all | bytes 2097152 | tf_op jit(solution)/shard_map/all_to_all | solution.py:44
  228.0 339.4 %all-gather.11.cloned.1.call-done = f32[32768,256]{1,0:T(8,128)} async-done(((f32[256,256]{1,0:T(8,128)}), f32[32768,256]{1,0:T(8,128)}) %all-gather.11.cloned.1.call-update) | async-done | bytes 33554448 | tf_op jit(solution)/shard_map/all_gather | solution.py:12
  567.4 12.2 %reduce_sum.99 = f32[256,256]{1,0:T(8,128)S(1)} reduce(f32[128,256,256]{2,1,0:T(8,128)} %bitcast.96, f32[]{:T(128)} %constant.80.clone.1), dimensions={0}, to_apply=%region_5.0 | reduce | flops 8323072 | bytes 33816580 | tf_op jit(solution)/shard_map/reduce_sum | solution.py:13
  579.8 11.7 cholesky.130
  591.6 9.8 custom-call.15
  601.9 11.7 cholesky.147
  619.9 30.9 %custom-call.16 = f32[2,128,128]{1,2,0:T(8,128)S(1)} custom-call(f32[2,128,128]{2,1,0:T(8,128)S(1)} %get-tuple-element.18), custom_call_target="InvertDiagBlocksLowerTriangular" | custom-call | tf_op jit(solution)/shard_map/jit(_solve_triangular)/triangular_solve | solution.py:108
  651.5 8.5 all_to_all.43
  660.2 22.4 %all_to_all.45 = f32[32,32,256]{2,1,0:T(8,128)S(1)} all-to-all(f32[32,32,256]{2,1,0:T(8,128)S(1)} %fusion.41), channel_id=1, replica_groups=mesh['grp'=4,'row'=32] {'row'}, dimensions={0} | all-to-all | bytes 2097152 | tf_op jit(solution)/shard_map/all_to_all | solution.py:44
  688.9 335.7 %all-gather.13.cloned.1.call-done = f32[32768,256]{1,0:T(8,128)} async-done(((f32[256,256]{1,0:T(8,128)}), f32[32768,256]{1,0:T(8,128)}) %all-gather.13.cloned.1.call-update) | async-done | bytes 33554448 | tf_op jit(solution)/shard_map/all_gather | solution.py:12
  1024.6 12.1 %reduce_sum.101 = f32[256,256]{1,0:T(8,128)S(1)} reduce(f32[128,256,256]{2,1,0:T(8,128)} %bitcast.97, f32[]{:T(128)} %constant.80.clone.1), dimensions={0}, to_apply=%region_11.14 | reduce | flops 8323072 | bytes 33816580 | tf_op jit(solution)/shard_map/reduce_sum | solution.py:13
  1036.9 11.7 cholesky.164
  1048.7 9.8 custom-call.17
  1059.0 11.7 cholesky.181
  1077.4 19.9 %custom-call.18 = f32[2,128,128]{1,2,0:T(8,128)S(1)} custom-call(f32[2,128,128]{2,1,0:T(8,128)S(1)} %get-tuple-element.19), custom_call_target="InvertDiagBlocksLowerTriangular" | custom-call | tf_op jit(solution)/shard_map/jit(_solve_triangular)/triangular_solve | solution.py:108
  1101.7 7.4 all-to-all-start.7
  1109.1 15.7 %fusion = (f32[4096]{0:T(1024)S(1)}, f32[1024,4096]{1,0:T(8,128)}) fusion(f32[4096]{0:T(1024)S(1)} %multiply_reduce_fusion, f32[1024]{0:T(1024)S(1)} %multiply_reduce_fusion.1, bf16[1024,1024]{1,0:T(8,128)(2,1)S(1)} %copy-done, bf16[4096,1024]{1,0:T(8,128)(2,1)} %all-gather.9.cloned.1.call-done), kind=kOutput, calls=%fused_computation.7 | convolution fusion | flops 8615096320 | bytes 27299840 | tf_op jit(solution)/shard_map/dot_general | solution.py:72
  1124.8 8.2 fusion.2
  1135.3 53.3 %reduce-scatter.2.cloned.1.call-done = f32[1024,257]{0,1:T(8,128)} async-done(((f32[4096,257]{0,1:T(8,128)}), f32[1024,257]{0,1:T(8,128)}) %reduce-scatter.2.cloned.1.call-update) | async-done | bytes 1052688 | tf_op jit(solution)/shard_map/reduce_scatter | solution.py:51
  (93 shorter events, 62.0 us)
Async XLA Ops:
  7.2 137.0 %all-gather.7.cloned.1.call-start = ((), (), s32[]{:S(2)}) async-start(), calls=%async_computation.9 | async-start | bytes 2162688 | tf_op jit(solution)/shard_map/all_gather | solution.py:91
  149.3 13.5 %all-to-all-start.1 = ((f32[32,1,1024]{2,1,0:T(1,128)}), f32[32,1,1024]{2,1,0:T(1,128)S(1)}, u32[]{:S(2)}, u32[]{:S(2)}) async-start(f32[32,1,1024]{2,1,0:T(1,128)} %broadcast_in_dim.15), calls=%async_computation.1 | async-start | bytes 262144 | tf_op jit(solution)/shard_map/all_to_all | solution.py:25
  163.6 32.6 %all-to-all-start.2 = ((f32[4,1,32]{2,1,0:T(1,128)}), f32[4,1,32]{2,1,0:T(1,128)S(1)}, u32[]{:S(2)}, u32[]{:S(2)}) async-start(f32[4,1,32]{2,1,0:T(1,128)} %broadcast_in_dim.16), calls=%async_computation.2 | async-start | bytes 4096 | tf_op jit(solution)/shard_map/all_to_all | solution.py:25
  197.6 8.7 all-to-all-start.3
  201.5 365.9 %all-gather.11.cloned.1.call-start = ((), (), s32[]{:S(2)}) async-start(), calls=%async_computation.12 | async-start | bytes 33816576 | tf_op jit(solution)/shard_map/all_gather | solution.py:12
  226.8 457.0 %all-gather.9.cloned.1.call-start = ((), (), s32[]{:S(2)}) async-start(), calls=%async_computation.10 | async-start | bytes 10485760 | tf_op jit(solution)/shard_map/all_gather | solution.py:114
  227.6 797.0 %all-gather.13.cloned.1.call-start = ((), (), s32[]{:S(2)}) async-start(), calls=%async_computation.13 | async-start | bytes 33816576 | tf_op jit(solution)/shard_map/all_gather | solution.py:12
  1024.6 84.5 %copy-start = (bf16[1024,1024]{1,0:T(8,128)(2,1)S(1)}, bf16[1024,1024]{1,0:T(8,128)(2,1)}, u32[]{:S(2)}) copy-start(bf16[1024,1024]{1,0:T(8,128)(2,1)} %all-gather.7.cloned.1.call-done) | copy-start | bytes 6291460
  1101.7 23.1 %all-to-all-start.7 = ((bf16[32,32,256]{2,1,0:T(8,128)(2,1)}), bf16[32,32,256]{2,1,0:T(8,128)(2,1)S(1)}, u32[]{:S(2)}, u32[]{:S(2)}) async-start(bf16[32,32,256]{2,1,0:T(8,128)(2,1)} %broadcast_in_dim.19), calls=%async_computation.7 | async-start | bytes 1048576 | tf_op jit(solution)/shard_map/all_to_all | solution.py:25
  1109.1 79.5 %reduce-scatter.2.cloned.1.call-start = ((), (), s32[]{:S(2)}) async-start(), calls=%async_computation.11 | async-start | bytes 5406720 | tf_op jit(solution)/shard_map/reduce_scatter | solution.py:51
Sparse Core Ops, SparseCore 0:
  9.6 134.4 all-gather.6
  227.0 340.4 all-gather.10
  569.1 63.3 all-gather.8
  683.9 340.6 all-gather.12
  1135.4 53.0 reduce-scatter.1
